TPU v7x, 256 devices: a 2x2x32 block of a 4x8x32 slice. The times are simulated.
256 devices in a mesh: groups: 4 (over x, y), tensor: 64 (over z, core).
Axes of the slice: x: 2, y: 2, z: 32, core: 2. Of those that a mesh axis runs over, the one named last changes fastest.
The devices are a block of a 4x8x32 slice.
Arguments:
- stem_field: float32 [16, 2, 1048576], P('groups', None, 'tensor'), parts along dimension 0, may hold values from -6 to 6
- branches: float32 [4, 2, 2, 256, 256], P(None, None, None, None, 'tensor'), may hold values from -0.25 to 0.25
- branch_order: int32 [4], replicated, may hold values from 0 to 3, each once
- slice_values: int32 [16, 4], P('groups'), parts along dimension 0, may hold values from 0 to 1
Outputs:
- amplitudes: float32 [8, 1048576], P('groups', 'tensor'), parts along dimension 0
There are 4 independent parts, one for each index of `groups`. A program takes and returns all parts, laid end to end along the dimension named above; an argument that names none is the same for every part. Nothing has to cross between parts.
Inputs may be any that keep to these rules, and one draw needn't show every extreme that they name: `branch_order`: each branch is merged exactly once.
All inputs are finite; a program needn't handle non-finite values.
Results may differ from a plain program's by a relative error of at most 0.00014.
Values sent between devices are 32-bit elements; how exact they have to be, the bound alone decides.
No kernel may reach another device: no remote copies, remote signals or barrier semaphores. Data moves between devices by JAX's collectives and lax.ppermute only.
A program may use at most 64 MiB of HBM per device.

v0:
```python
import functools

import jax
import jax.numpy as jnp
from jax import lax
from jax.experimental import pallas as pl
from jax.experimental.pallas import tpu as pltpu
from jax.sharding import PartitionSpec as P


LANES = 128
HALF = LANES // 2
PRECISION = lax.Precision.HIGH


def dot_t(left, right):
    return lax.dot_general(
        left, right, (((1,), (1,)), ((), ())), precision=PRECISION, preferred_element_type=jnp.float32
    )


def dot(left, right):
    return lax.dot_general(
        left, right, (((1,), (0,)), ((), ())), precision=PRECISION, preferred_element_type=jnp.float32
    )


def low_lanes(rows):
    return lax.broadcasted_iota(jnp.int32, (rows, LANES), 1) < HALF


def put_table(table, piece, row, chips, parity, core):
    for value in range(2):
        at = row + 16 * value
        real, imag = piece[:, at : at + 8, :], piece[:, at + 8 : at + 16, :]
        low = lax.broadcasted_iota(jnp.int32, real.shape, 1) < 4
        real_r, imag_r = pltpu.roll(real, 4, 1), pltpu.roll(imag, 4, 1)
        columns = (
            jnp.where(low, real, imag_r),
            jnp.where(low, real_r, imag),
            jnp.where(low, -imag, real_r),
            jnp.where(low, -imag_r, real),
        )
        for spot, column in enumerate(columns):
            at = (4 * value + spot) * LANES
            table[chips, parity, core, :, at : at + LANES] = column


def put_tables(pieces, tables):
    place = lax.axis_index("tensor")
    core = lax.rem(place, 2)
    parity = lax.rem(place // 2, 2)
    chips = pieces[0].shape[0]
    for step, table in enumerate(tables):
        for (own, up, down), c in ((pieces[:3], core), (pieces[3:], 1 - core)):
            put_table(table, own, 32 * step, slice(0, chips), parity, c)
            put_table(table, up, 32 * step, slice(0, chips // 2), 1 - parity, c)
            put_table(table, down, 32 * step, slice(chips // 2, chips), 1 - parity, c)


def flat(table):
    return table[...].reshape(-1, table.shape[-1])


def put_rows(masked, x, row, column, chosen):
    rows, at, other = x.shape[0], column * LANES, (4 + column) * LANES
    zero = jnp.zeros_like(x)
    masked[row : row + rows, at : at + LANES] = jnp.where(chosen, zero, x)
    masked[row : row + rows, other : other + LANES] = jnp.where(chosen, x, zero)


def pick_kernel(first, order, block, after, out):
    rows = block.shape[1]
    for t in range(2):
        out[t * rows : (t + 1) * rows, :] = block[order[first + t]]


def first_kernel(values, stem, *refs):
    pieces, (after, out, one, two, masked, state) = refs[:6], refs[6:]
    put_tables(pieces, (one, two))
    slices = values.shape[0]
    middle = stem.shape[0] // (4 * slices)
    for s in range(slices):
        for column in range(4):
            part, half = divmod(column, 2)
            x = stem[pl.ds(4 * middle * s + 2 * half + part, middle, stride=4), :]
            put_rows(masked, x, middle * s, column, values[s, 0] == 1)
    merged = dot_t(flat(one), masked[...])
    for pair in range(slices // 2):
        state[pair] = merged[:, pair * LANES : (pair + 1) * LANES]
    count = merged.shape[0] // 8
    low = low_lanes(count)
    for pair in range(slices // 2):
        for column in range(4):
            a = state[pair, pl.ds(2 * column, count, stride=8), :]
            b = state[pair, pl.ds(2 * column + 1, count, stride=8), :]
            even = jnp.where(low, a, pltpu.roll(b, HALF, 1))
            odd = jnp.where(low, pltpu.roll(a, HALF, 1), b)
            put_rows(masked, even, count * 2 * pair, column, values[2 * pair, 1] == 1)
            put_rows(masked, odd, count * (2 * pair + 1), column, values[2 * pair + 1, 1] == 1)
    merged = dot_t(flat(two), masked[...])
    for pair in range(slices // 2):
        x = merged[:, pair * LANES : (pair + 1) * LANES]
        out[:, 8 * pair : 8 * pair + 8, :] = x.reshape(count, 8, LANES)


def table_kernel(*refs):
    put_tables(refs[:6], refs[6:])


def second_kernel(values, moved, three, four, out, masked, sums, right, last):
    slices = values.shape[0]
    pairs = slices // 2
    count = moved.shape[0] // (8 * pairs)
    low = low_lanes(count)

    def picked(pair, step, rows):
        in_low = low_lanes(rows)
        return (in_low & (values[2 * pair, step] == 1)) | (~in_low & (values[2 * pair + 1, step] == 1))

    for pair in range(pairs):
        at = pair * LANES
        one = picked(pair, 2, count)
        for j in range(8):
            x = moved[pl.ds(8 * pair + j, count, stride=8 * pairs), :]
            zero = jnp.zeros_like(x)
            masked[count * j : count * (j + 1), at : at + LANES] = jnp.where(one, zero, x)
            masked[count * (8 + j) : count * (9 + j), at : at + LANES] = jnp.where(one, x, zero)
    merged = dot(flat(three), masked[...])
    for value in range(2):
        total = jnp.zeros((merged.shape[0], LANES), jnp.float32)
        for pair in range(pairs):
            x = merged[:, pair * LANES : (pair + 1) * LANES]
            one = picked(pair, 3, merged.shape[0])
            total = total + (jnp.where(one, x, 0.0) if value else jnp.where(one, 0.0, x))
        sums[value] = total + pltpu.roll(total, HALF, 1)
    for value in range(2):
        for column in range(4):
            a = sums[value, pl.ds(2 * column, count, stride=8), :]
            b = sums[value, pl.ds(2 * column + 1, count, stride=8), :]
            x = jnp.where(low, a, b)
            at = (4 * value + column) * LANES
            right[0:count, at : at + LANES] = x
            right[count : 2 * count, at : at + LANES] = x
    last[...] = dot_t(flat(four), right[...])
    for column in range(4):
        a = last[pl.ds(2 * column, count, stride=8), :]
        b = last[pl.ds(2 * column + 1, count, stride=8), :]
        out[pl.ds(column, count, stride=4), :] = jnp.where(low, a, b)


def last_kernel(moved, out):
    count = moved.shape[0] // 4
    low = low_lanes(count)
    for part in range(2):
        rows = [moved[pl.ds(2 * part + half, count, stride=4), :] for half in range(2)]
        turned = jnp.concatenate(rows, axis=0).T
        first, second = turned[:count], turned[count:]
        out[pl.ds(part, count, stride=4), :] = jnp.where(low, first, pltpu.roll(second, HALF, 1))
        out[pl.ds(2 + part, count, stride=4), :] = jnp.where(low, pltpu.roll(first, HALF, 1), second)


def local_call(kernel, out_shape, scratch, spaces, flops):
    kinds = {"s": pltpu.SMEM, "v": pltpu.VMEM, "a": pl.ANY}
    specs = [pl.BlockSpec(memory_space=kinds[space]) for space in spaces]
    vmem = pl.BlockSpec(memory_space=pltpu.VMEM)
    many = isinstance(out_shape, list)
    shapes = [jax.ShapeDtypeStruct(shape, jnp.float32) for shape in (out_shape if many else [out_shape])]
    return pl.pallas_call(
        kernel,
        out_shape=shapes if many else shapes[0],
        in_specs=specs,
        out_specs=[vmem] * len(shapes) if many else vmem,
        scratch_shapes=[pltpu.VMEM(shape, jnp.float32) for shape in scratch],
        cost_estimate=pl.CostEstimate(flops=flops, bytes_accessed=4 * 2**20, transcendentals=0),
        compiler_params=pltpu.CompilerParams(vmem_limit_bytes=24 * 2**20),
    )


def gather_same_core(block, shards):
    rings = [[core + 2 * (start + 2 * i) for i in range(shards // 4)] for start in range(2) for core in range(2)]
    return lax.all_gather(block, "tensor", axis_index_groups=rings)


def spread(own, shards):
    half = own.shape[0] // 2
    lower, upper = own[:half], own[half:]
    sent = []
    for x, chips, cross in ((lower, 1, 0), (upper, -1, 0), (own, 0, 1), (lower, 1, 1), (upper, -1, 1)):
        pairs = [(i, ((i + 2 * chips) % shards) ^ cross) for i in range(shards)]
        sent.append(lax.ppermute(x, "tensor", pairs))
    return (own, *sent)


def per_device(stem_field, branches, branch_order, slice_values):
    shards = lax.axis_size("tensor")
    slices, parts, entries = stem_field.shape
    steps, n_values, _, contract, width = branches.shape
    middle = entries // contract
    halves = contract // LANES
    block = branches.transpose(0, 1, 2, 4, 3).reshape(steps, n_values, parts, width, halves, LANES)
    block = block.transpose(0, 1, 2, 4, 3, 5).reshape(steps, n_values * parts * halves * width, LANES)

    def pick(first, after):
        shape = (2 * block.shape[1], LANES)
        kernel = functools.partial(pick_kernel, first)
        return local_call(kernel, shape, [], "sva", 1000)(branch_order, block, after)

    stem = stem_field.reshape(slices, parts, middle * halves, LANES).transpose(0, 2, 1, 3).reshape(-1, LANES)
    first = gather_same_core(pick(0, slice_values), shards)
    later = gather_same_core(pick(2, first), shards)
    ordered = later
    first, later = spread(first, shards), spread(later, shards)

    rows = shards * 2 * width
    deep = n_values * parts * contract
    table = (shards // 4, 2, 2, 2 * width, deep)
    lanes = slices * middle
    flops = 2 * 2 * rows * deep * lanes
    merged = local_call(
        first_kernel,
        (shards, 8 * slices // 2, LANES),
        [table, table, (lanes, deep), (slices // 2, rows, LANES)],
        "svvvvvvva",
        flops,
    )(slice_values, stem, *first, ordered)
    moved = lax.all_to_all(merged, "tensor", split_axis=0, concat_axis=0, tiled=True)
    tables = local_call(table_kernel, [table, table], [], "vvvvvv", 1000)(*later)
    summed = local_call(
        second_kernel,
        (shards * 4, LANES),
        [(deep, lanes), (2, rows, LANES), (2 * middle, deep), (rows, LANES)],
        "svvv",
        flops,
    )(slice_values, moved.reshape(-1, LANES), *tables)
    final = lax.all_to_all(summed.reshape(shards, 4, LANES), "tensor", split_axis=0, concat_axis=0, tiled=True)
    out = local_call(last_kernel, (middle * halves * parts, LANES), [], "v", 1000)(final.reshape(-1, LANES))
    return out.reshape(middle * halves, parts, LANES).transpose(1, 0, 2).reshape(parts, entries)


def solution(mesh):
    return jax.shard_map(
        per_device,
        mesh=mesh,
        in_specs=(
            P("groups", None, "tensor"),
            P(None, None, None, None, "tensor"),
            P(),
            P("groups", None),
        ),
        out_specs=P("groups", "tensor"),
        check_vma=False,
    )
```

profile of v0, /device:TPU:37, one launch (start us, length us, event | category | flops | bytes accessed | tf_op | source)
XLA Modules:
  0.0 245.7 jit_solution(3728217472265688034)
XLA Ops:
  0.0 0.0 copy-start.2
  0.0 0.0 copy-start.3
  0.0 0.9 copy-done.3
  0.9 0.0 copy-start.4
  0.9 0.7 copy-done.4
  1.6 0.0 copy-start.6
  1.6 0.7 copy-done.6
  2.2 0.0 copy-start.5
  2.2 0.5 shard_map.46
  2.8 49.6 %all-gather = f32[1024,128]{1,0:T(8,128)S(1)} all-gather(f32[64,128]{1,0:T(8,128)S(1)} %shard_map.46), channel_id=2, replica_groups={{0,4,8,12,16,20,24,28,32,36,40,44,48,52,56,60},{1,5,9,13,17,21,25,29,33..., dimensions={0}, use_global_device_ids=true | all-gather | bytes 557056 | tf_op jit(solution)/shard_map/all_gather | solution.py:182
  52.4 7.9 %collective-permute-start.2 = (f32[16,64,128]{2,1,0:T(8,128)S(1)}, f32[16,64,128]{2,1,0:T(8,128)S(1)}, u32[]{:S(2)}, u32[]{:S(2)}) collective-permute-start(f32[16,64,128]{2,1,0:T(8,128)S(1)} %bitcast.26), channel_id=1, source_target_pairs={{0,1},{1,0},{2,3},{3,2},{4,5},{5,4},{6,7},{7,6},{8,9},{9,8},{10,11... | collective-permute-start | bytes 1572872 | tf_op jit(solution)/shard_map/ppermute | solution.py:191
  60.3 1.9 collective-permute-start.3
  62.2 0.2 collective-permute-start
  62.4 3.1 %collective-permute-start.4 = (f32[8,64,128]{2,1,0:T(8,128)S(1)}, f32[8,64,128]{2,1,0:T(8,128)S(1)}, u32[]{:S(2)}, u32[]{:S(2)}) collective-permute-start(f32[8,64,128]{2,1,0:T(8,128)S(1)} %bitcast.38), channel_id=1, source_target_pairs={{0,63},{1,62},{2,1},{3,0},{4,3},{5,2},{6,5},{7,4},{8,7},{9,6},{10,... | collective-permute-start | bytes 786440 | tf_op jit(solution)/shard_map/ppermute | solution.py:191
  65.5 0.0 collective-permute-start.1
  65.5 0.5 shard_map.47
  66.1 37.6 %all-gather.1 = f32[1024,128]{1,0:T(8,128)S(1)} all-gather(f32[64,128]{1,0:T(8,128)S(1)} %shard_map.47), channel_id=3, replica_groups={{0,4,8,12,16,20,24,28,32,36,40,44,48,52,56,60},{1,5,9,13,17,21,25,29,33..., dimensions={0}, use_global_device_ids=true | all-gather | bytes 557056 | tf_op jit(solution)/shard_map/all_gather | solution.py:182
  103.7 0.0 collective-permute-done.3.refs_4_
  103.7 0.0 collective-permute-done.refs_1_
  103.7 0.0 collective-permute-done.4.refs_5_
  103.7 0.0 collective-permute-done.1.refs_2_
  103.7 0.0 collective-permute-done.2.refs_3_
  103.7 0.0 copy-done.2
  103.7 0.0 copy-done.5
  103.7 5.7 %shard_map.48 = f32[64,16,128]{2,1,0:T(8,128)} custom-call(s32[4,4]{1,0:T(4,128)S(1)} %copy-done.5, f32[1024,128]{1,0:T(8,128)S(1)} %bitcast.33, f32[16,64,128]{2,1,0:T(8,128)S(1)} %bitcast.28, f32[8,64,128]{2,1,0:T(8,128)S(1)} %collective-permute-done.refs_1_, f32[8,64,128]{2,1,0:T(8,128)S(1)} %collective-permute-done.1.refs_2_, ...), custom_call_target="tpu_custom_call" | custom-call | flops 536870912 | bytes 4194304 | tf_op jit(solution)/shard_map/pallas_call | solution.py:220
  109.4 18.1 %all-to-all-start = ((f32[64,16,128]{2,1,0:T(8,128)}), f32[64,16,128]{2,1,0:T(8,128)S(1)}, u32[]{:S(2)}, u32[]{:S(2)}) async-start(f32[64,16,128]{2,1,0:T(8,128)} %shard_map.48), calls=%async_computation | async-start | bytes 1048576 | tf_op jit(solution)/shard_map/all_to_all | solution.py:227
  127.5 1.4 collective-permute-start.7
  129.0 0.5 collective-permute-start.8
  129.5 1.2 collective-permute-start.5
  130.7 2.1 collective-permute-start.9
  132.7 1.0 collective-permute-start.6
  133.8 48.0 %collective-permute-done.8.refs_4_ = f32[8,64,128]{2,1,0:T(8,128)S(1)} collective-permute-done((f32[8,64,128]{2,1,0:T(8,128)S(1)}, f32[8,64,128]{2,1,0:T(8,128)S(1)}, u32[]{:S(2)}, u32[]{:S(2)}) %collective-permute-start.8) | collective-permute-done | bytes 262176 | tf_op jit(solution)/shard_map/ppermute | solution.py:191
  181.8 4.9 %collective-permute-done.5.refs_1_ = f32[8,64,128]{2,1,0:T(8,128)S(1)} collective-permute-done((f32[8,64,128]{2,1,0:T(8,128)S(1)}, f32[8,64,128]{2,1,0:T(8,128)S(1)}, u32[]{:S(2)}, u32[]{:S(2)}) %collective-permute-start.5) | collective-permute-done | bytes 262176 | tf_op jit(solution)/shard_map/ppermute | solution.py:191
  186.7 0.0 collective-permute-done.9.refs_5_
  186.7 0.0 collective-permute-done.6.refs_2_
  186.7 0.0 collective-permute-done.7.refs_3_
  186.7 0.3 shard_map.49
  187.1 0.0 copy-start
  187.1 1.3 copy-done
  188.4 2.7 %all-to-all-done = f32[64,16,128]{2,1,0:T(8,128)S(1)} async-done(((f32[64,16,128]{2,1,0:T(8,128)}), f32[64,16,128]{2,1,0:T(8,128)S(1)}, u32[]{:S(2)}, u32[]{:S(2)}) %all-to-all-start) | async-done | bytes 524320 | tf_op jit(solution)/shard_map/all_to_all | solution.py:227
  191.0 0.0 copy-start.1
  191.0 1.6 copy-done.1
  192.6 4.3 %shard_map.50 = f32[256,128]{1,0:T(8,128)S(1)} custom-call(s32[4,4]{1,0:T(4,128)S(1)} %copy-done.5, f32[1024,128]{1,0:T(8,128)S(1)} %bitcast.32, f32[16,2,2,8,1024]{4,3,2,1,0:T(8,128)S(1)} %get-tuple-element.7.three, f32[16,2,2,8,1024]{4,3,2,1,0:T(8,128)S(1)} %copy-done.1), custom_call_target="tpu_custom_call" | custom-call | flops 536870912 | bytes 4194304 | tf_op jit(solution)/shard_map/pallas_call | solution.py:229
  196.9 48.0 %all_to_all.10 = f32[64,4,128]{2,1,0:T(4,128)S(1)} all-to-all(f32[64,4,128]{2,1,0:T(4,128)S(1)} %bitcast.34), channel_id=1, replica_groups=mesh['groups'=4,'tensor'=64] {'tensor'}, dimensions={0} | all-to-all | bytes 262144 | tf_op jit(solution)/shard_map/all_to_all | solution.py:236
  244.9 0.8 shard_map.51
  (2 shorter events, 0.1 us)
Async XLA Ops:
  0.0 103.7 %copy-start.2 = (f32[4,2,16384]{2,1,0:T(2,128)S(1)}, f32[4,2,16384]{2,1,0:T(2,128)}, u32[]{:S(2)}) copy-start(f32[4,2,16384]{2,1,0:T(2,128)} %param.4) | copy-start | bytes 1572868
  0.0 0.9 copy-start.3
  0.9 0.7 copy-start.4
  1.6 0.7 copy-start.6
  2.2 101.5 %copy-start.5 = (s32[4,4]{1,0:T(4,128)S(1)}, s32[4,4]{1,0:T(4,128)}, u32[]{:S(2)}) copy-start(s32[4,4]{1,0:T(4,128)} %values.3) | copy-start | bytes 196
  52.4 51.4 %collective-permute-start.2 = (f32[16,64,128]{2,1,0:T(8,128)S(1)}, f32[16,64,128]{2,1,0:T(8,128)S(1)}, u32[]{:S(2)}, u32[]{:S(2)}) collective-permute-start(f32[16,64,128]{2,1,0:T(8,128)S(1)} %bitcast.26), channel_id=1, source_target_pairs={{0,1},{1,0},{2,3},{3,2},{4,5},{5,4},{6,7},{7,6},{8,9},{9,8},{10,11... | collective-permute-start | bytes 1572872 | tf_op jit(solution)/shard_map/ppermute | solution.py:191
  60.3 43.4 %collective-permute-start.3 = (f32[8,64,128]{2,1,0:T(8,128)S(1)}, f32[8,64,128]{2,1,0:T(8,128)S(1)}, u32[]{:S(2)}, u32[]{:S(2)}) collective-permute-start(f32[8,64,128]{2,1,0:T(8,128)S(1)} %bitcast.42), channel_id=1, source_target_pairs={{0,3},{1,2},{2,5},{3,4},{4,7},{5,6},{6,9},{7,8},{8,11},{9,10},{10,... | collective-permute-start | bytes 786440 | tf_op jit(solution)/shard_map/ppermute | solution.py:191
  62.2 41.5 %collective-permute-start = (f32[8,64,128]{2,1,0:T(8,128)S(1)}, f32[8,64,128]{2,1,0:T(8,128)S(1)}, u32[]{:S(2)}, u32[]{:S(2)}) collective-permute-start(f32[8,64,128]{2,1,0:T(8,128)S(1)} %bitcast.43), channel_id=1, source_target_pairs={{0,2},{1,3},{2,4},{3,5},{4,6},{5,7},{6,8},{7,9},{8,10},{9,11},{10,... | collective-permute-start | bytes 786440 | tf_op jit(solution)/shard_map/ppermute | solution.py:191
  62.4 41.2 %collective-permute-start.4 = (f32[8,64,128]{2,1,0:T(8,128)S(1)}, f32[8,64,128]{2,1,0:T(8,128)S(1)}, u32[]{:S(2)}, u32[]{:S(2)}) collective-permute-start(f32[8,64,128]{2,1,0:T(8,128)S(1)} %bitcast.38), channel_id=1, source_target_pairs={{0,63},{1,62},{2,1},{3,0},{4,3},{5,2},{6,5},{7,4},{8,7},{9,6},{10,... | collective-permute-start | bytes 786440 | tf_op jit(solution)/shard_map/ppermute | solution.py:191
  65.5 38.1 %collective-permute-start.1 = (f32[8,64,128]{2,1,0:T(8,128)S(1)}, f32[8,64,128]{2,1,0:T(8,128)S(1)}, u32[]{:S(2)}, u32[]{:S(2)}) collective-permute-start(f32[8,64,128]{2,1,0:T(8,128)S(1)} %bitcast.39), channel_id=1, source_target_pairs={{0,62},{1,63},{2,0},{3,1},{4,2},{5,3},{6,4},{7,5},{8,6},{9,7},{10,... | collective-permute-start | bytes 786440 | tf_op jit(solution)/shard_map/ppermute | solution.py:191
  109.4 81.6 %all-to-all-start = ((f32[64,16,128]{2,1,0:T(8,128)}), f32[64,16,128]{2,1,0:T(8,128)S(1)}, u32[]{:S(2)}, u32[]{:S(2)}) async-start(f32[64,16,128]{2,1,0:T(8,128)} %shard_map.48), calls=%async_computation | async-start | bytes 1048576 | tf_op jit(solution)/shard_map/all_to_all | solution.py:227
  127.5 59.3 %collective-permute-start.7 = (f32[16,64,128]{2,1,0:T(8,128)S(1)}, f32[16,64,128]{2,1,0:T(8,128)S(1)}, u32[]{:S(2)}, u32[]{:S(2)}) collective-permute-start(f32[16,64,128]{2,1,0:T(8,128)S(1)} %bitcast.30), channel_id=1, source_target_pairs={{0,1},{1,0},{2,3},{3,2},{4,5},{5,4},{6,7},{7,6},{8,9},{9,8},{10,11... | collective-permute-start | bytes 1572872 | tf_op jit(solution)/shard_map/ppermute | solution.py:191
  129.0 52.8 %collective-permute-start.8 = (f32[8,64,128]{2,1,0:T(8,128)S(1)}, f32[8,64,128]{2,1,0:T(8,128)S(1)}, u32[]{:S(2)}, u32[]{:S(2)}) collective-permute-start(f32[8,64,128]{2,1,0:T(8,128)S(1)} %bitcast.44), channel_id=1, source_target_pairs={{0,3},{1,2},{2,5},{3,4},{4,7},{5,6},{6,9},{7,8},{8,11},{9,10},{10,... | collective-permute-start | bytes 786440 | tf_op jit(solution)/shard_map/ppermute | solution.py:191
  129.5 57.2 %collective-permute-start.5 = (f32[8,64,128]{2,1,0:T(8,128)S(1)}, f32[8,64,128]{2,1,0:T(8,128)S(1)}, u32[]{:S(2)}, u32[]{:S(2)}) collective-permute-start(f32[8,64,128]{2,1,0:T(8,128)S(1)} %bitcast.45), channel_id=1, source_target_pairs={{0,2},{1,3},{2,4},{3,5},{4,6},{5,7},{6,8},{7,9},{8,10},{9,11},{10,... | collective-permute-start | bytes 786440 | tf_op jit(solution)/shard_map/ppermute | solution.py:191
  130.7 56.1 %collective-permute-start.9 = (f32[8,64,128]{2,1,0:T(8,128)S(1)}, f32[8,64,128]{2,1,0:T(8,128)S(1)}, u32[]{:S(2)}, u32[]{:S(2)}) collective-permute-start(f32[8,64,128]{2,1,0:T(8,128)S(1)} %bitcast.40), channel_id=1, source_target_pairs={{0,63},{1,62},{2,1},{3,0},{4,3},{5,2},{6,5},{7,4},{8,7},{9,6},{10,... | collective-permute-start | bytes 786440 | tf_op jit(solution)/shard_map/ppermute | solution.py:191
  132.7 54.0 %collective-permute-start.6 = (f32[8,64,128]{2,1,0:T(8,128)S(1)}, f32[8,64,128]{2,1,0:T(8,128)S(1)}, u32[]{:S(2)}, u32[]{:S(2)}) collective-permute-start(f32[8,64,128]{2,1,0:T(8,128)S(1)} %bitcast.41), channel_id=1, source_target_pairs={{0,62},{1,63},{2,0},{3,1},{4,2},{5,3},{6,4},{7,5},{8,6},{9,7},{10,... | collective-permute-start | bytes 786440 | tf_op jit(solution)/shard_map/ppermute | solution.py:191
  187.1 1.3 copy-start
  191.0 1.6 copy-start.1
where the time goes:
time: 246 us
  blocking collectives  135 us (55%)
  waiting for transfers between devices  55.6 us (23%)
  starting transfers between devices  37.5 us (15%)
  Pallas kernels  12.2 us (5%)
  local copies, waits for them, and re-layouts  5.23 us (2%)
    all_gather x2, blocking collectives, gather_same_core(): return lax.all_gather(block, 'tensor', axis_index_groups=rings)  87.1 us
    ppermute x10, waiting for transfers between devices, spread(): sent.append(lax.ppermute(x, 'tensor', pairs))  53 us
    all_to_all x1, blocking collectives, per_device(): lax.all_to_all(summed.reshape(shards, 4, LANES), 'tensor', split_axis=0,...  48 us
    ppermute x10, starting transfers between devices, spread(): sent.append(lax.ppermute(x, 'tensor', pairs))  19.4 us
    all_to_all x1, starting transfers between devices, per_device(): lax.all_to_all(merged, 'tensor', split_axis=0, concat_axis=0, tiled=True)  18.1 us
    pallas_call x1, Pallas kernels, per_device(): local_call(first_kernel, (shards, 8 * slices // 2, LANES), [table, table,...  5.67 us
    unnamed x14, local copies, waits for them, and re-layouts  5.16 us
  transfers between devices with their start and end apart: 11, of which 3 were waited for; matrix products, arithmetic and copies ran while one was open for 0% of the time, Pallas kernels for 0%

commit v1 on v0

--- a/solution.py
+++ b/solution.py
@@ -1,5 +1,3 @@
-import functools
-
 import jax
 import jax.numpy as jnp
 from jax import lax
@@ -46,10 +44,13 @@
             table[chips, parity, core, :, at : at + LANES] = column
 
 
-def put_tables(pieces, tables):
+def core_and_parity():
     place = lax.axis_index("tensor")
-    core = lax.rem(place, 2)
-    parity = lax.rem(place // 2, 2)
+    return lax.rem(place, 2), lax.rem(place // 2, 2)
+
+
+def put_first(pieces, tables):
+    core, parity = core_and_parity()
     chips = pieces[0].shape[0]
     for step, table in enumerate(tables):
         for (own, up, down), c in ((pieces[:3], core), (pieces[3:], 1 - core)):
@@ -58,6 +59,15 @@
             put_table(table, down, 32 * step, slice(chips // 2, chips), 1 - parity, c)
 
 
+def table_kernel(own, other, *tables):
+    core, _ = core_and_parity()
+    chips = own.shape[0]
+    for step, table in enumerate(tables):
+        for piece, c in ((own, core), (other, 1 - core)):
+            for parity in range(2):
+                put_table(table, piece.at[:, parity], 32 * step, slice(0, chips), parity, c)
+
+
 def flat(table):
     return table[...].reshape(-1, table.shape[-1])
 
@@ -69,15 +79,16 @@
     masked[row : row + rows, other : other + LANES] = jnp.where(chosen, x, zero)
 
 
-def pick_kernel(first, order, block, after, out):
+def pick_kernel(order, block, *outs):
     rows = block.shape[1]
-    for t in range(2):
-        out[t * rows : (t + 1) * rows, :] = block[order[first + t]]
+    for k, out in enumerate(outs):
+        for t in range(2):
+            out[t * rows : (t + 1) * rows, :] = block[order[2 * k + t]]
 
 
 def first_kernel(values, stem, *refs):
-    pieces, (after, out, one, two, masked, state) = refs[:6], refs[6:]
-    put_tables(pieces, (one, two))
+    pieces, (out, one, two, masked, state) = refs[:6], refs[6:]
+    put_first(pieces, (one, two))
     slices = values.shape[0]
     middle = stem.shape[0] // (4 * slices)
     for s in range(slices):
@@ -102,10 +113,6 @@
     for pair in range(slices // 2):
         x = merged[:, pair * LANES : (pair + 1) * LANES]
         out[:, 8 * pair : 8 * pair + 8, :] = x.reshape(count, 8, LANES)
-
-
-def table_kernel(*refs):
-    put_tables(refs[:6], refs[6:])
 
 
 def second_kernel(values, moved, three, four, out, masked, sums, right, last):
@@ -177,19 +184,16 @@
     )
 
 
-def gather_same_core(block, shards):
+def send(x, shards, chips, cross):
+    return lax.ppermute(x, "tensor", [(i, ((i + 2 * chips) % shards) ^ cross) for i in range(shards)])
+
+
+def exchange(block, shards):
     rings = [[core + 2 * (start + 2 * i) for i in range(shards // 4)] for start in range(2) for core in range(2)]
-    return lax.all_gather(block, "tensor", axis_index_groups=rings)
-
-
-def spread(own, shards):
+    own = lax.all_gather(block, "tensor", axis_index_groups=rings)
     half = own.shape[0] // 2
-    lower, upper = own[:half], own[half:]
-    sent = []
-    for x, chips, cross in ((lower, 1, 0), (upper, -1, 0), (own, 0, 1), (lower, 1, 1), (upper, -1, 1)):
-        pairs = [(i, ((i + 2 * chips) % shards) ^ cross) for i in range(shards)]
-        sent.append(lax.ppermute(x, "tensor", pairs))
-    return (own, *sent)
+    up, down = send(own[:half], shards, 1, 0), send(own[half:], shards, -1, 0)
+    return own, up, down, send(own, shards, 0, 1), send(up, shards, 0, 1), send(down, shards, 0, 1)
 
 
 def per_device(stem_field, branches, branch_order, slice_values):
@@ -201,16 +205,13 @@
     block = branches.transpose(0, 1, 2, 4, 3).reshape(steps, n_values, parts, width, halves, LANES)
     block = block.transpose(0, 1, 2, 4, 3, 5).reshape(steps, n_values * parts * halves * width, LANES)
 
-    def pick(first, after):
-        shape = (2 * block.shape[1], LANES)
-        kernel = functools.partial(pick_kernel, first)
-        return local_call(kernel, shape, [], "sva", 1000)(branch_order, block, after)
-
     stem = stem_field.reshape(slices, parts, middle * halves, LANES).transpose(0, 2, 1, 3).reshape(-1, LANES)
-    first = gather_same_core(pick(0, slice_values), shards)
-    later = gather_same_core(pick(2, first), shards)
-    ordered = later
-    first, later = spread(first, shards), spread(later, shards)
+    picked = (2 * block.shape[1], LANES)
+    first, later = local_call(pick_kernel, [picked, picked], [], "sv", 1000)(branch_order, block)
+    cores = [[core + 2 * i for i in range(shards // 2)] for core in range(2)]
+    later = lax.all_gather(later, "tensor", axis_index_groups=cores).reshape(shards // 4, 2, *picked)
+    swapped = send(later, shards, 0, 1)
+    first = exchange(first, shards)
 
     rows = shards * 2 * width
     deep = n_values * parts * contract
@@ -221,11 +222,11 @@
         first_kernel,
         (shards, 8 * slices // 2, LANES),
         [table, table, (lanes, deep), (slices // 2, rows, LANES)],
-        "svvvvvvva",
+        "svvvvvvv",
         flops,
-    )(slice_values, stem, *first, ordered)
+    )(slice_values, stem, *first)
     moved = lax.all_to_all(merged, "tensor", split_axis=0, concat_axis=0, tiled=True)
-    tables = local_call(table_kernel, [table, table], [], "vvvvvv", 1000)(*later)
+    tables = local_call(table_kernel, [table, table], [], "vv", 1000)(later, swapped)
     summed = local_call(
         second_kernel,
         (shards * 4, LANES),

time: 246 us -> 301 us (1.22)
  waiting for transfers between devices: 55.6 us -> 125 us
  blocking collectives: 135 us -> 93.5 us
  between operations: 0.11 us -> 13.5 us
  starting transfers between devices: 37.5 us -> 48.5 us
    all_gather x0 -> x1, waiting for transfers between devices: none -> 121 us  [per_device(): lax.all_gather(later, 'tensor', axis_index_groups=cores)]
    ppermute x10 -> x6, waiting for transfers between devices: 53 us -> 3.67 us  [send(): lax.ppermute(x, 'tensor', [(i, (i + 2 * chips) % shards ^ cross) for i in...]
    all_gather x2 -> x1, blocking collectives: 87.1 us -> 49.5 us  [exchange(): own = lax.all_gather(block, 'tensor', axis_index_groups=rings)]
    ppermute x10 -> x6, starting transfers between devices: 19.4 us -> 35.8 us  [send(): lax.ppermute(x, 'tensor', [(i, (i + 2 * chips) % shards ^ cross) for i in...]
    all_to_all x1, starting transfers between devices: 18.1 us -> 12.6 us  [per_device(): lax.all_to_all(merged, 'tensor', split_axis=0, concat_axis=0, tiled=True)]
    all_to_all x1, blocking collectives: 48 us -> 44 us  [per_device(): lax.all_to_all(summed.reshape(shards, 4, LANES), 'tensor', split_axis=0,...]
    unnamed x14 -> x16, local copies, waits for them, and re-layouts: 5.16 us -> 7.36 us
  transfers between devices with their start and end apart: 11 -> 8, of which waited for: 3 -> 4; matrix products, arithmetic and copies ran while one was open for 0% -> 0% of each run, Pallas kernels for 0% -> 0%
where the time goes in v1:
time: 301 us; the launch traced here: 300 us
  waiting for transfers between devices  125 us (42%)
  blocking collectives  93.5 us (31%)
  starting transfers between devices  48.5 us (16%)
  between operations  13.5 us (4%)
  Pallas kernels  12.4 us (4%)
  local copies, waits for them, and re-layouts  7.4 us (2%)
    all_gather x1, waiting for transfers between devices, per_device(): lax.all_gather(later, 'tensor', axis_index_groups=cores)  121 us
    all_gather x1, blocking collectives, exchange(): own = lax.all_gather(block, 'tensor', axis_index_groups=rings)  49.5 us
    all_to_all x1, blocking collectives, per_device(): lax.all_to_all(summed.reshape(shards, 4, LANES), 'tensor', split_axis=0,...  44 us
    ppermute x6, starting transfers between devices, send(): lax.ppermute(x, 'tensor', [(i, (i + 2 * chips) % shards ^ cross) for i in...  35.8 us
    all_to_all x1, starting transfers between devices, per_device(): lax.all_to_all(merged, 'tensor', split_axis=0, concat_axis=0, tiled=True)  12.6 us
    unnamed x16, local copies, waits for them, and re-layouts  7.36 us
  transfers between devices with their start and end apart: 8, of which 4 were waited for; matrix products, arithmetic and copies ran while one was open for 0% of the time, Pallas kernels for 0%

profile of v1, /device:TPU:37, one launch (start us, length us, event | category | flops | bytes accessed | tf_op | source)
XLA Modules:
  0.0 300.5 jit_solution(11960670132766107215)
XLA Ops:
  6.5 0.0 copy-start.4
  6.5 0.8 copy-done.4
  7.4 0.0 copy-start.7
  7.4 0.7 copy-done.7
  8.0 1.2 shard_map.46
  9.2 49.5 %all-gather = f32[1024,128]{1,0:T(8,128)S(1)} all-gather(f32[64,128]{1,0:T(8,128)S(1)} %get-tuple-element.9), channel_id=2, replica_groups={{0,4,8,12,16,20,24,28,32,36,40,44,48,52,56,60},{1,5,9,13,17,21,25,29,33..., dimensions={0}, use_global_device_ids=true | all-gather | bytes 557056 | tf_op jit(solution)/shard_map/all_gather | solution.py:193
  58.8 1.9 collective-permute-start
  60.6 0.9 collective-permute-start.1
  61.6 8.7 %collective-permute-start.2 = (f32[16,64,128]{2,1,0:T(8,128)S(1)}, f32[16,64,128]{2,1,0:T(8,128)S(1)}, u32[]{:S(2)}, u32[]{:S(2)}) collective-permute-start(f32[16,64,128]{2,1,0:T(8,128)S(1)} %bitcast.24), channel_id=1, source_target_pairs={{0,1},{1,0},{2,3},{3,2},{4,5},{5,4},{6,7},{7,6},{8,9},{9,8},{10,11... | collective-permute-start | bytes 1572872 | tf_op jit(solution)/shard_map/ppermute | solution.py:188
  70.3 0.0 collective-permute-done.refs_1_
  70.3 4.3 %collective-permute-start.3 = (f32[8,64,128]{2,1,0:T(8,128)S(1)}, f32[8,64,128]{2,1,0:T(8,128)S(1)}, u32[]{:S(2)}, u32[]{:S(2)}) collective-permute-start(f32[8,64,128]{2,1,0:T(8,128)S(1)} %collective-permute-done.refs_1_), channel_id=1, source_target_pairs={{0,1},{1,0},{2,3},{3,2},{4,5},{5,4},{6,7},{7,6},{8,9},{9,8},{10,11... | collective-permute-start | bytes 786440 | tf_op jit(solution)/shard_map/ppermute | solution.py:188
  74.6 0.0 collective-permute-done.1.refs_2_
  74.6 0.7 collective-permute-start.4
  75.3 0.4 collective-permute-done.3.refs_4_
  75.8 0.7 collective-permute-done.4.refs_5_
  76.5 0.0 collective-permute-done.2.refs_3_
  76.5 0.0 copy-start.3
  76.5 1.0 copy-done.3
  77.5 0.0 copy-start.5
  77.5 0.7 copy-done.5
  78.2 5.7 %shard_map.47 = f32[64,16,128]{2,1,0:T(8,128)} custom-call(s32[4,4]{1,0:T(4,128)S(1)} %copy-done.5, f32[1024,128]{1,0:T(8,128)S(1)} %bitcast.31, f32[16,64,128]{2,1,0:T(8,128)S(1)} %bitcast.25, f32[8,64,128]{2,1,0:T(8,128)S(1)} %collective-permute-done.refs_1_, f32[8,64,128]{2,1,0:T(8,128)S(1)} %collective-permute-done.1.refs_2_, ...), custom_call_target="tpu_custom_call" | custom-call | flops 536870912 | bytes 4194304 | tf_op jit(solution)/shard_map/pallas_call | solution.py:221
  83.9 0.0 copy-start.6
  83.9 12.6 %all-to-all-start = ((f32[64,16,128]{2,1,0:T(8,128)}), f32[64,16,128]{2,1,0:T(8,128)S(1)}, u32[]{:S(2)}, u32[]{:S(2)}) async-start(f32[64,16,128]{2,1,0:T(8,128)} %shard_map.47), calls=%async_computation | async-start | bytes 1048576 | tf_op jit(solution)/shard_map/all_to_all | solution.py:228
  96.6 0.1 all-gather.4.cloned.1.call-start
  96.6 0.7 all-gather.4.cloned.1.call-update
  97.4 120.8 %all-gather.4.cloned.1.call-done = f32[2048,128]{1,0:T(8,128)} async-done(((f32[64,128]{1,0:T(8,128)}), f32[2048,128]{1,0:T(8,128)}) %all-gather.4.cloned.1.call-update) | async-done | bytes 1048592 | tf_op jit(solution)/shard_map/all_gather | solution.py:212
  218.2 19.2 %collective-permute-start.5 = (f32[16,2,64,128]{3,2,1,0:T(8,128)}, f32[16,2,64,128]{3,2,1,0:T(8,128)S(1)}, u32[]{:S(2)}, u32[]{:S(2)}) collective-permute-start(f32[16,2,64,128]{3,2,1,0:T(8,128)} %bitcast.27), channel_id=1, source_target_pairs={{0,1},{1,0},{2,3},{3,2},{4,5},{5,4},{6,7},{7,6},{8,9},{9,8},{10,11... | collective-permute-start | bytes 3145736 | tf_op jit(solution)/shard_map/ppermute | solution.py:188
  237.4 2.5 collective-permute-done.5.other
  239.9 0.0 copy-start.2
  239.9 1.2 copy-done.2
  241.1 0.4 shard_map.48
  241.6 0.0 copy-start
  241.6 1.3 copy-done
  242.9 0.0 all-to-all-done
  242.9 0.0 copy-done.6
  242.9 0.0 copy-start.1
  242.9 1.6 copy-done.1
  244.5 4.3 %shard_map.49 = f32[256,128]{1,0:T(8,128)S(1)} custom-call(s32[4,4]{1,0:T(4,128)S(1)} %copy-done.6, f32[1024,128]{1,0:T(8,128)S(1)} %bitcast.26, f32[16,2,2,8,1024]{4,3,2,1,0:T(8,128)S(1)} %get-tuple-element.11.three, f32[16,2,2,8,1024]{4,3,2,1,0:T(8,128)S(1)} %copy-done.1), custom_call_target="tpu_custom_call" | custom-call | flops 536870912 | bytes 4194304 | tf_op jit(solution)/shard_map/pallas_call | solution.py:230
  248.8 44.0 %all_to_all.10 = f32[64,4,128]{2,1,0:T(4,128)S(1)} all-to-all(f32[64,4,128]{2,1,0:T(4,128)S(1)} %bitcast.29), channel_id=1, replica_groups=mesh['groups'=4,'tensor'=64] {'tensor'}, dimensions={0} | all-to-all | bytes 262144 | tf_op jit(solution)/shard_map/all_to_all | solution.py:237
  292.8 0.8 shard_map.50
  (1 shorter events, 0.0 us)
Async XLA Ops:
  6.5 0.8 copy-start.4
  7.4 0.7 copy-start.7
  58.8 11.5 %collective-permute-start = (f32[8,64,128]{2,1,0:T(8,128)S(1)}, f32[8,64,128]{2,1,0:T(8,128)S(1)}, u32[]{:S(2)}, u32[]{:S(2)}) collective-permute-start(f32[8,64,128]{2,1,0:T(8,128)S(1)} %bitcast.34), channel_id=1, source_target_pairs={{0,2},{1,3},{2,4},{3,5},{4,6},{5,7},{6,8},{7,9},{8,10},{9,11},{10,... | collective-permute-start | bytes 786440 | tf_op jit(solution)/shard_map/ppermute | solution.py:188
  60.6 14.0 %collective-permute-start.1 = (f32[8,64,128]{2,1,0:T(8,128)S(1)}, f32[8,64,128]{2,1,0:T(8,128)S(1)}, u32[]{:S(2)}, u32[]{:S(2)}) collective-permute-start(f32[8,64,128]{2,1,0:T(8,128)S(1)} %bitcast.33), channel_id=1, source_target_pairs={{0,62},{1,63},{2,0},{3,1},{4,2},{5,3},{6,4},{7,5},{8,6},{9,7},{10,... | collective-permute-start | bytes 786440 | tf_op jit(solution)/shard_map/ppermute | solution.py:188
  61.6 14.9 %collective-permute-start.2 = (f32[16,64,128]{2,1,0:T(8,128)S(1)}, f32[16,64,128]{2,1,0:T(8,128)S(1)}, u32[]{:S(2)}, u32[]{:S(2)}) collective-permute-start(f32[16,64,128]{2,1,0:T(8,128)S(1)} %bitcast.24), channel_id=1, source_target_pairs={{0,1},{1,0},{2,3},{3,2},{4,5},{5,4},{6,7},{7,6},{8,9},{9,8},{10,11... | collective-permute-start | bytes 1572872 | tf_op jit(solution)/shard_map/ppermute | solution.py:188
  70.3 5.5 %collective-permute-start.3 = (f32[8,64,128]{2,1,0:T(8,128)S(1)}, f32[8,64,128]{2,1,0:T(8,128)S(1)}, u32[]{:S(2)}, u32[]{:S(2)}) collective-permute-start(f32[8,64,128]{2,1,0:T(8,128)S(1)} %collective-permute-done.refs_1_), channel_id=1, source_target_pairs={{0,1},{1,0},{2,3},{3,2},{4,5},{5,4},{6,7},{7,6},{8,9},{9,8},{10,11... | collective-permute-start | bytes 786440 | tf_op jit(solution)/shard_map/ppermute | solution.py:188
  74.6 1.9 collective-permute-start.4
  76.5 1.0 copy-start.3
  77.5 0.7 copy-start.5
  83.9 159.0 %copy-start.6 = (s32[4,4]{1,0:T(4,128)S(1)}, s32[4,4]{1,0:T(4,128)}, u32[]{:S(2)}) copy-start(s32[4,4]{1,0:T(4,128)} %values.3) | copy-start | bytes 196
  83.9 159.0 %all-to-all-start = ((f32[64,16,128]{2,1,0:T(8,128)}), f32[64,16,128]{2,1,0:T(8,128)S(1)}, u32[]{:S(2)}, u32[]{:S(2)}) async-start(f32[64,16,128]{2,1,0:T(8,128)} %shard_map.47), calls=%async_computation | async-start | bytes 1048576 | tf_op jit(solution)/shard_map/all_to_all | solution.py:228
  96.6 121.6 %all-gather.4.cloned.1.call-start = ((), (), s32[]{:S(2)}) async-start(), calls=%async_computation.2 | async-start | bytes 1081344 | tf_op jit(solution)/shard_map/all_gather | solution.py:212
  218.2 21.7 %collective-permute-start.5 = (f32[16,2,64,128]{3,2,1,0:T(8,128)}, f32[16,2,64,128]{3,2,1,0:T(8,128)S(1)}, u32[]{:S(2)}, u32[]{:S(2)}) collective-permute-start(f32[16,2,64,128]{3,2,1,0:T(8,128)} %bitcast.27), channel_id=1, source_target_pairs={{0,1},{1,0},{2,3},{3,2},{4,5},{5,4},{6,7},{7,6},{8,9},{9,8},{10,11... | collective-permute-start | bytes 3145736 | tf_op jit(solution)/shard_map/ppermute | solution.py:188
  239.9 1.2 copy-start.2
  241.6 1.3 copy-start
  242.9 1.6 copy-start.1
Sparse Core Ops, SparseCore 0:
  99.2 118.9 all-gather.3

commit v2 on v1

--- a/solution.py
+++ b/solution.py
@@ -49,54 +49,74 @@
     return lax.rem(place, 2), lax.rem(place // 2, 2)
 
 
-def put_first(pieces, tables):
-    core, parity = core_and_parity()
-    chips = pieces[0].shape[0]
-    for step, table in enumerate(tables):
-        for (own, up, down), c in ((pieces[:3], core), (pieces[3:], 1 - core)):
-            put_table(table, own, 32 * step, slice(0, chips), parity, c)
-            put_table(table, up, 32 * step, slice(0, chips // 2), 1 - parity, c)
-            put_table(table, down, 32 * step, slice(chips // 2, chips), 1 - parity, c)
-
-
-def table_kernel(own, other, *tables):
-    core, _ = core_and_parity()
-    chips = own.shape[0]
-    for step, table in enumerate(tables):
-        for piece, c in ((own, core), (other, 1 - core)):
-            for parity in range(2):
-                put_table(table, piece.at[:, parity], 32 * step, slice(0, chips), parity, c)
-
-
 def flat(table):
     return table[...].reshape(-1, table.shape[-1])
 
 
-def put_rows(masked, x, row, column, chosen):
+def put_rows(masked, x, row, column, flag):
     rows, at, other = x.shape[0], column * LANES, (4 + column) * LANES
+    chosen = jnp.broadcast_to(flag, x.shape) == 1
     zero = jnp.zeros_like(x)
     masked[row : row + rows, at : at + LANES] = jnp.where(chosen, zero, x)
     masked[row : row + rows, other : other + LANES] = jnp.where(chosen, x, zero)
 
 
-def pick_kernel(order, block, *outs):
+def pick_kernel(order_in, block_in, out, order, block, sems):
+    copies = [
+        pltpu.make_async_copy(order_in, order, sems.at[0]),
+        pltpu.make_async_copy(block_in, block, sems.at[1]),
+    ]
+    for copy in copies:
+        copy.start()
+    for copy in copies:
+        copy.wait()
     rows = block.shape[1]
-    for k, out in enumerate(outs):
-        for t in range(2):
-            out[t * rows : (t + 1) * rows, :] = block[order[2 * k + t]]
-
-
-def first_kernel(values, stem, *refs):
-    pieces, (out, one, two, masked, state) = refs[:6], refs[6:]
-    put_first(pieces, (one, two))
-    slices = values.shape[0]
+    for k, t in enumerate((0, 1, 2 + turn())):
+        out[k * rows : (k + 1) * rows, :] = block[order[t]]
+
+
+def turn():
+    return lax.rem(lax.axis_index("groups"), 2)
+
+
+def core_and_parity():
+    place = lax.axis_index("tensor")
+    return lax.rem(place, 2), lax.rem(place // 2, 2)
+
+
+def spots(pieces):
+    core, parity = core_and_parity()
+    chips = pieces[0].shape[0]
+    for (own, up, down), c in ((pieces[:3], core), (pieces[3:], 1 - core)):
+        yield own, slice(0, chips), parity, c
+        yield up, slice(0, chips // 2), 1 - parity, c
+        yield down, slice(chips // 2, chips), 1 - parity, c
+
+
+def stem_kernel(values, stem, masked, flags):
+    slices, steps = values.shape
+    for t in range(steps):
+        for s in range(slices):
+            flags[t * slices + s : t * slices + s + 1, :] = jnp.full((1, LANES), values[s, t], jnp.int32)
+        for pair in range(slices // 2):
+            row = slices * steps + t * (slices // 2) + pair
+            flags[row : row + 1, :] = jnp.where(low_lanes(1), values[2 * pair, t], values[2 * pair + 1, t])
     middle = stem.shape[0] // (4 * slices)
     for s in range(slices):
         for column in range(4):
             part, half = divmod(column, 2)
             x = stem[pl.ds(4 * middle * s + 2 * half + part, middle, stride=4), :]
-            put_rows(masked, x, middle * s, column, values[s, 0] == 1)
-    merged = dot_t(flat(one), masked[...])
+            put_rows(masked, x, middle * s, column, flags[s : s + 1, :])
+
+
+def first_kernel(flags, start, *refs):
+    pieces, (out, mine, one, two, masked, state) = refs[:6], refs[6:]
+    for piece, chips, parity, core in spots(pieces):
+        for step, table in enumerate((one, two)):
+            put_table(table, piece, 32 * step, chips, parity, core)
+        mine[chips, parity, core] = piece[:, 64:, :]
+    slices = out.shape[1] // 4
+    merged = dot_t(flat(one), start[...])
     for pair in range(slices // 2):
         state[pair] = merged[:, pair * LANES : (pair + 1) * LANES]
     count = merged.shape[0] // 8
@@ -107,23 +127,27 @@
             b = state[pair, pl.ds(2 * column + 1, count, stride=8), :]
             even = jnp.where(low, a, pltpu.roll(b, HALF, 1))
             odd = jnp.where(low, pltpu.roll(a, HALF, 1), b)
-            put_rows(masked, even, count * 2 * pair, column, values[2 * pair, 1] == 1)
-            put_rows(masked, odd, count * (2 * pair + 1), column, values[2 * pair + 1, 1] == 1)
+            put_rows(masked, even, count * 2 * pair, column, flags[slices + 2 * pair : slices + 2 * pair + 1, :])
+            put_rows(masked, odd, count * (2 * pair + 1), column, flags[slices + 2 * pair + 1 : slices + 2 * pair + 2, :])
     merged = dot_t(flat(two), masked[...])
     for pair in range(slices // 2):
         x = merged[:, pair * LANES : (pair + 1) * LANES]
         out[:, 8 * pair : 8 * pair + 8, :] = x.reshape(count, 8, LANES)
 
 
-def second_kernel(values, moved, three, four, out, masked, sums, right, last):
-    slices = values.shape[0]
-    pairs = slices // 2
+def second_kernel(flags, moved, mine, other, out, tables, masked, sums, right, last):
+    for piece, spot in ((mine, turn()), (other, 1 - turn())):
+        for k in range(4):
+            parity, core = divmod(k, 2)
+            put_table(tables.at[spot], piece.at[:, parity, core], 0, slice(0, piece.shape[0]), parity, core)
+    three, four = tables.at[0], tables.at[1]
+    pairs = masked.shape[1] // LANES
     count = moved.shape[0] // (8 * pairs)
     low = low_lanes(count)
 
     def picked(pair, step, rows):
-        in_low = low_lanes(rows)
-        return (in_low & (values[2 * pair, step] == 1)) | (~in_low & (values[2 * pair + 1, step] == 1))
+        row = flags.shape[0] // 6 * 4 + step * pairs + pair
+        return jnp.broadcast_to(flags[row : row + 1, :], (rows, LANES)) == 1
 
     for pair in range(pairs):
         at = pair * LANES
@@ -167,12 +191,12 @@
         out[pl.ds(2 + part, count, stride=4), :] = jnp.where(low, pltpu.roll(first, HALF, 1), second)
 
 
-def local_call(kernel, out_shape, scratch, spaces, flops):
-    kinds = {"s": pltpu.SMEM, "v": pltpu.VMEM, "a": pl.ANY}
+def local_call(kernel, out_shape, scratch, spaces, flops, kinds_out=(jnp.float32,)):
+    kinds = {"s": pltpu.SMEM, "v": pltpu.VMEM}
     specs = [pl.BlockSpec(memory_space=kinds[space]) for space in spaces]
     vmem = pl.BlockSpec(memory_space=pltpu.VMEM)
     many = isinstance(out_shape, list)
-    shapes = [jax.ShapeDtypeStruct(shape, jnp.float32) for shape in (out_shape if many else [out_shape])]
+    shapes = [jax.ShapeDtypeStruct(*out) for out in zip(out_shape if many else [out_shape], kinds_out, strict=True)]
     return pl.pallas_call(
         kernel,
         out_shape=shapes if many else shapes[0],
@@ -192,7 +216,8 @@
     rings = [[core + 2 * (start + 2 * i) for i in range(shards // 4)] for start in range(2) for core in range(2)]
     own = lax.all_gather(block, "tensor", axis_index_groups=rings)
     half = own.shape[0] // 2
-    up, down = send(own[:half], shards, 1, 0), send(own[half:], shards, -1, 0)
+    up = send(own[:half], shards, 1, 0)
+    down = send(own[half:], shards, -1, 0)
     return own, up, down, send(own, shards, 0, 1), send(up, shards, 0, 1), send(down, shards, 0, 1)
 
 
@@ -206,34 +231,46 @@
     block = block.transpose(0, 1, 2, 4, 3, 5).reshape(steps, n_values * parts * halves * width, LANES)
 
     stem = stem_field.reshape(slices, parts, middle * halves, LANES).transpose(0, 2, 1, 3).reshape(-1, LANES)
-    picked = (2 * block.shape[1], LANES)
-    first, later = local_call(pick_kernel, [picked, picked], [], "sv", 1000)(branch_order, block)
-    cores = [[core + 2 * i for i in range(shards // 2)] for core in range(2)]
-    later = lax.all_gather(later, "tensor", axis_index_groups=cores).reshape(shards // 4, 2, *picked)
-    swapped = send(later, shards, 0, 1)
-    first = exchange(first, shards)
+    part_rows = block.shape[1]
+    picked = pl.pallas_call(
+        pick_kernel,
+        out_shape=jax.ShapeDtypeStruct((3 * part_rows, LANES), jnp.float32),
+        in_specs=[pl.BlockSpec(memory_space=pl.ANY)] * 2,
+        out_specs=pl.BlockSpec(memory_space=pltpu.VMEM),
+        scratch_shapes=[
+            pltpu.SMEM((steps,), jnp.int32),
+            pltpu.VMEM(block.shape, jnp.float32),
+            pltpu.SemaphoreType.DMA((2,)),
+        ],
+    )(branch_order, block)
+    pieces = exchange(picked, shards)
 
     rows = shards * 2 * width
     deep = n_values * parts * contract
     table = (shards // 4, 2, 2, 2 * width, deep)
     lanes = slices * middle
     flops = 2 * 2 * rows * deep * lanes
-    merged = local_call(
+    pairs = slices // 2
+    start, flags = local_call(
+        stem_kernel, [(lanes, deep), ((slices + pairs) * steps, LANES)], [], "sv", 10**8, (jnp.float32, jnp.int32)
+    )(slice_values, stem)
+    merged, mine = local_call(
         first_kernel,
-        (shards, 8 * slices // 2, LANES),
-        [table, table, (lanes, deep), (slices // 2, rows, LANES)],
-        "svvvvvvv",
+        [(shards, 8 * pairs, LANES), (shards // 4, 2, 2, part_rows, LANES)],
+        [table, table, (lanes, deep), (pairs, rows, LANES)],
+        "v" * 8,
         flops,
-    )(slice_values, stem, *first)
+        (jnp.float32, jnp.float32),
+    )(flags, start, *pieces)
     moved = lax.all_to_all(merged, "tensor", split_axis=0, concat_axis=0, tiled=True)
-    tables = local_call(table_kernel, [table, table], [], "vv", 1000)(later, swapped)
+    other = lax.ppermute(mine, "groups", [(g, g ^ 1) for g in range(lax.axis_size("groups"))])
     summed = local_call(
         second_kernel,
         (shards * 4, LANES),
-        [(deep, lanes), (2, rows, LANES), (2 * middle, deep), (rows, LANES)],
-        "svvv",
+        [(2, *table), (deep, lanes), (2, rows, LANES), (2 * middle, deep), (rows, LANES)],
+        "vvvv",
         flops,
-    )(slice_values, moved.reshape(-1, LANES), *tables)
+    )(flags, moved.reshape(-1, LANES), mine, other)
     final = lax.all_to_all(summed.reshape(shards, 4, LANES), "tensor", split_axis=0, concat_axis=0, tiled=True)
     out = local_call(last_kernel, (middle * halves * parts, LANES), [], "v", 1000)(final.reshape(-1, LANES))
     return out.reshape(middle * halves, parts, LANES).transpose(1, 0, 2).reshape(parts, entries)

time: 301 us -> 199 us (0.66)
  waiting for transfers between devices: 125 us -> 63.4 us
  starting transfers between devices: 48.5 us -> 32.5 us
  between operations: 13.5 us -> 0.05 us
  local copies, waits for them, and re-layouts: 7.4 us -> 0.06 us
  blocking collectives: 93.5 us -> 90.4 us
    all_gather x1 -> x0, waiting for transfers between devices: 121 us -> none  [per_device(): lax.all_gather(later, 'tensor', axis_index_groups=cores)]
    all_to_all x1, waiting for transfers between devices: 0.01 us -> 40.1 us  [per_device(): lax.all_to_all(merged, 'tensor', split_axis=0, concat_axis=0, tiled=True)]
    ppermute x0 -> x1, waiting for transfers between devices: none -> 22 us  [per_device(): lax.ppermute(mine, 'groups', [(g, g ^ 1) for g in range(lax.axis_size('gr...]
    ppermute x6 -> x5, starting transfers between devices: 35.8 us -> 18.8 us  [send(): lax.ppermute(x, 'tensor', [(i, (i + 2 * chips) % shards ^ cross) for i in...]
    unnamed x16 -> x4, local copies, waits for them, and re-layouts: 7.36 us -> 0.01 us
    all_to_all x1, blocking collectives: 44 us -> 36.9 us  [per_device(): lax.all_to_all(summed.reshape(shards, 4, LANES), 'tensor', split_axis=0,...]
    all_gather x1, blocking collectives: 49.5 us -> 53.6 us  [exchange(): own = lax.all_gather(block, 'tensor', axis_index_groups=rings)]
  transfers between devices with their start and end apart: 8 -> 7, of which waited for: 4 -> 4; matrix products, arithmetic and copies ran while one was open for 0% -> 0% of each run, Pallas kernels for 0% -> 0%
where the time goes in v2:
time: 199 us
  blocking collectives  90.4 us (45%)
  waiting for transfers between devices  63.4 us (32%)
  starting transfers between devices  32.5 us (16%)
  Pallas kernels  12.6 us (6%)
    all_gather x1, blocking collectives, exchange(): own = lax.all_gather(block, 'tensor', axis_index_groups=rings)  53.6 us
    all_to_all x1, waiting for transfers between devices, per_device(): lax.all_to_all(merged, 'tensor', split_axis=0, concat_axis=0, tiled=True)  40.1 us
    all_to_all x1, blocking collectives, per_device(): lax.all_to_all(summed.reshape(shards, 4, LANES), 'tensor', split_axis=0,...  36.9 us
    ppermute x1, waiting for transfers between devices, per_device(): lax.ppermute(mine, 'groups', [(g, g ^ 1) for g in range(lax.axis_size('gr...  22 us
    ppermute x5, starting transfers between devices, send(): lax.ppermute(x, 'tensor', [(i, (i + 2 * chips) % shards ^ cross) for i in...  18.8 us
    all_to_all x1, starting transfers between devices, per_device(): lax.all_to_all(merged, 'tensor', split_axis=0, concat_axis=0, tiled=True)  11.9 us
    pallas_call x1, Pallas kernels, per_device(): local_call(first_kernel, [(shards, 8 * pairs, LANES), (shards // 4, 2, 2,...  5.11 us
    pallas_call x1, Pallas kernels, per_device(): local_call(second_kernel, (shards * 4, LANES), [(2, *table), (deep, lanes...  4.52 us
  transfers between devices with their start and end apart: 7, of which 4 were waited for; matrix products, arithmetic and copies ran while one was open for 0% of the time, Pallas kernels for 0%

profile of v2, /device:TPU:37, one launch (start us, length us, event | category | flops | bytes accessed | tf_op | source)
XLA Modules:
  0.0 199.0 jit_solution(6565044915359803033)
XLA Ops:
  0.0 1.5 shard_map.47
  1.5 53.6 %all-gather = f32[1536,128]{1,0:T(8,128)S(1)} all-gather(f32[96,128]{1,0:T(8,128)} %shard_map.47), channel_id=2, replica_groups={{0,4,8,12,16,20,24,28,32,36,40,44,48,52,56,60},{1,5,9,13,17,21,25,29,33..., dimensions={0}, use_global_device_ids=true | all-gather | bytes 835584 | tf_op jit(solution)/shard_map/all_gather | solution.py:217
  55.1 0.0 copy-start
  55.1 0.1 fusion
  55.1 2.2 %collective-permute-start = (f32[8,96,128]{2,1,0:T(8,128)S(1)}, f32[8,96,128]{2,1,0:T(8,128)S(1)}, u32[]{:S(2)}, u32[]{:S(2)}) collective-permute-start(f32[8,96,128]{2,1,0:T(8,128)S(1)} %bitcast.30), channel_id=1, source_target_pairs={{0,2},{1,3},{2,4},{3,5},{4,6},{5,7},{6,8},{7,9},{8,10},{9,11},{10,... | collective-permute-start | bytes 1179656 | tf_op jit(solution)/shard_map/ppermute | solution.py:212
  57.3 0.0 copy-start.1
  57.3 0.6 collective-permute-start.1
  57.9 10.2 %collective-permute-start.2 = (f32[16,96,128]{2,1,0:T(8,128)S(1)}, f32[16,96,128]{2,1,0:T(8,128)S(1)}, u32[]{:S(2)}, u32[]{:S(2)}) collective-permute-start(f32[16,96,128]{2,1,0:T(8,128)S(1)} %bitcast.23), channel_id=1, source_target_pairs={{0,1},{1,0},{2,3},{3,2},{4,5},{5,4},{6,7},{7,6},{8,9},{9,8},{10,11... | collective-permute-start | bytes 2359304 | tf_op jit(solution)/shard_map/ppermute | solution.py:212
  68.1 0.0 collective-permute-done.refs_1_
  68.1 5.7 %collective-permute-start.3 = (f32[8,96,128]{2,1,0:T(8,128)S(1)}, f32[8,96,128]{2,1,0:T(8,128)S(1)}, u32[]{:S(2)}, u32[]{:S(2)}) collective-permute-start(f32[8,96,128]{2,1,0:T(8,128)S(1)} %collective-permute-done.refs_1_), channel_id=1, source_target_pairs={{0,1},{1,0},{2,3},{3,2},{4,5},{5,4},{6,7},{7,6},{8,9},{9,8},{10,11... | collective-permute-start | bytes 1179656 | tf_op jit(solution)/shard_map/ppermute | solution.py:212
  73.9 0.0 collective-permute-done.1.refs_2_
  73.9 0.0 collective-permute-start.4
  73.9 0.0 copy-done
  73.9 0.0 copy-done.1
  73.9 0.7 shard_map.46
  74.6 0.6 collective-permute-done.3.refs_4_
  75.2 0.6 collective-permute-done.4.refs_5_
  75.8 0.0 collective-permute-done.2.refs_3_
  75.8 5.1 %shard_map.48 = (f32[64,16,128]{2,1,0:T(8,128)}, f32[16,2,2,32,128]{4,3,2,1,0:T(8,128)S(1)}) custom-call(s32[24,128]{1,0:T(8,128)S(1)} %get-tuple-element.9.flags, f32[256,1024]{1,0:T(8,128)S(1)} %get-tuple-element.10.start, f32[16,96,128]{2,1,0:T(8,128)S(1)} %bitcast.24, f32[8,96,128]{2,1,0:T(8,128)S(1)} %collective-permute-done.refs_1_, ...), custom_call_target="tpu_custom_call" | custom-call | flops 536870912 | bytes 4194304 | tf_op jit(solution)/shard_map/pallas_call | solution.py:257
  80.9 11.9 %all-to-all-start = ((f32[64,16,128]{2,1,0:T(8,128)}), f32[64,16,128]{2,1,0:T(8,128)S(1)}, u32[]{:S(2)}, u32[]{:S(2)}) async-start(f32[64,16,128]{2,1,0:T(8,128)} %get-tuple-element.11), calls=%async_computation | async-start | bytes 1048576 | tf_op jit(solution)/shard_map/all_to_all | solution.py:265
  92.8 1.8 collective-permute-start.5
  94.6 22.0 %collective-permute-done.5.other = f32[16,2,2,32,128]{4,3,2,1,0:T(8,128)S(1)} collective-permute-done((f32[16,2,2,32,128]{4,3,2,1,0:T(8,128)S(1)}, f32[16,2,2,32,128]{4,3,2,1,0:T(8,128)S(1)}, u32[]{:S(2)}, u32[]{:S(2)}) %collective-permute-start.5) | collective-permute-done | bytes 1048608 | tf_op jit(solution)/shard_map/ppermute | solution.py:266
  116.7 40.1 %all-to-all-done = f32[64,16,128]{2,1,0:T(8,128)S(1)} async-done(((f32[64,16,128]{2,1,0:T(8,128)}), f32[64,16,128]{2,1,0:T(8,128)S(1)}, u32[]{:S(2)}, u32[]{:S(2)}) %all-to-all-start) | async-done | bytes 524320 | tf_op jit(solution)/shard_map/all_to_all | solution.py:265
  156.8 4.5 %shard_map.49 = f32[256,128]{1,0:T(8,128)S(1)} custom-call(s32[24,128]{1,0:T(8,128)S(1)} %get-tuple-element.9.flags, f32[1024,128]{1,0:T(8,128)S(1)} %bitcast.25, f32[16,2,2,32,128]{4,3,2,1,0:T(8,128)S(1)} %get-tuple-element.12.mine, f32[16,2,2,32,128]{4,3,2,1,0:T(8,128)S(1)} %collective-permute-done.5.other), custom_call_target="tpu_custom_call" | custom-call | flops 536870912 | bytes 4194304 | tf_op jit(solution)/shard_map/pallas_call | solution.py:267
  161.3 36.9 %all_to_all.10 = f32[64,4,128]{2,1,0:T(4,128)S(1)} all-to-all(f32[64,4,128]{2,1,0:T(4,128)S(1)} %bitcast.28), channel_id=1, replica_groups=mesh['groups'=4,'tensor'=64] {'tensor'}, dimensions={0} | all-to-all | bytes 262144 | tf_op jit(solution)/shard_map/all_to_all | solution.py:274
  198.2 0.8 shard_map.50
Async XLA Ops:
  55.1 18.8 %copy-start = (f32[4,2,16384]{2,1,0:T(2,128)S(1)}, f32[4,2,16384]{2,1,0:T(2,128)}, u32[]{:S(2)}) copy-start(f32[4,2,16384]{2,1,0:T(2,128)} %param.4) | copy-start | bytes 1572868
  55.1 13.0 %collective-permute-start = (f32[8,96,128]{2,1,0:T(8,128)S(1)}, f32[8,96,128]{2,1,0:T(8,128)S(1)}, u32[]{:S(2)}, u32[]{:S(2)}) collective-permute-start(f32[8,96,128]{2,1,0:T(8,128)S(1)} %bitcast.30), channel_id=1, source_target_pairs={{0,2},{1,3},{2,4},{3,5},{4,6},{5,7},{6,8},{7,9},{8,10},{9,11},{10,... | collective-permute-start | bytes 1179656 | tf_op jit(solution)/shard_map/ppermute | solution.py:212
  57.3 16.6 %copy-start.1 = (s32[4,4]{1,0:T(4,128)S(1)}, s32[4,4]{1,0:T(4,128)}, u32[]{:S(2)}) copy-start(s32[4,4]{1,0:T(4,128)} %values.1) | copy-start | bytes 196
  57.3 16.6 %collective-permute-start.1 = (f32[8,96,128]{2,1,0:T(8,128)S(1)}, f32[8,96,128]{2,1,0:T(8,128)S(1)}, u32[]{:S(2)}, u32[]{:S(2)}) collective-permute-start(f32[8,96,128]{2,1,0:T(8,128)S(1)} %bitcast.29), channel_id=1, source_target_pairs={{0,62},{1,63},{2,0},{3,1},{4,2},{5,3},{6,4},{7,5},{8,6},{9,7},{10,... | collective-permute-start | bytes 1179656 | tf_op jit(solution)/shard_map/ppermute | solution.py:212
  57.9 17.9 %collective-permute-start.2 = (f32[16,96,128]{2,1,0:T(8,128)S(1)}, f32[16,96,128]{2,1,0:T(8,128)S(1)}, u32[]{:S(2)}, u32[]{:S(2)}) collective-permute-start(f32[16,96,128]{2,1,0:T(8,128)S(1)} %bitcast.23), channel_id=1, source_target_pairs={{0,1},{1,0},{2,3},{3,2},{4,5},{5,4},{6,7},{7,6},{8,9},{9,8},{10,11... | collective-permute-start | bytes 2359304 | tf_op jit(solution)/shard_map/ppermute | solution.py:212
  68.1 7.1 %collective-permute-start.3 = (f32[8,96,128]{2,1,0:T(8,128)S(1)}, f32[8,96,128]{2,1,0:T(8,128)S(1)}, u32[]{:S(2)}, u32[]{:S(2)}) collective-permute-start(f32[8,96,128]{2,1,0:T(8,128)S(1)} %collective-permute-done.refs_1_), channel_id=1, source_target_pairs={{0,1},{1,0},{2,3},{3,2},{4,5},{5,4},{6,7},{7,6},{8,9},{9,8},{10,11... | collective-permute-start | bytes 1179656 | tf_op jit(solution)/shard_map/ppermute | solution.py:212
  73.9 1.9 collective-permute-start.4
  80.9 75.9 %all-to-all-start = ((f32[64,16,128]{2,1,0:T(8,128)}), f32[64,16,128]{2,1,0:T(8,128)S(1)}, u32[]{:S(2)}, u32[]{:S(2)}) async-start(f32[64,16,128]{2,1,0:T(8,128)} %get-tuple-element.11), calls=%async_computation | async-start | bytes 1048576 | tf_op jit(solution)/shard_map/all_to_all | solution.py:265
  92.8 23.8 %collective-permute-start.5 = (f32[16,2,2,32,128]{4,3,2,1,0:T(8,128)S(1)}, f32[16,2,2,32,128]{4,3,2,1,0:T(8,128)S(1)}, u32[]{:S(2)}, u32[]{:S(2)}) collective-permute-start(f32[16,2,2,32,128]{4,3,2,1,0:T(8,128)S(1)} %get-tuple-element.12.mine), channel_id=1, source_target_pairs={{0,64},{64,0},{128,192},{192,128},{1,65},{65,1},{129,193},{193,129... | collective-permute-start | bytes 3145736 | tf_op jit(solution)/shard_map/ppermute | solution.py:266

commit v3 on v2

--- a/solution.py
+++ b/solution.py
@@ -8,18 +8,21 @@
 
 LANES = 128
 HALF = LANES // 2
-PRECISION = lax.Precision.HIGH
-
-
-def dot_t(left, right):
+
+
+def split(x):
+    high = x.astype(jnp.bfloat16)
+    return high, (x - high.astype(jnp.float32)).astype(jnp.bfloat16)
+
+
+def product(left, right, axis):
+    left_high, left_low = split(left)
+    right_high, right_low = split(right)
     return lax.dot_general(
-        left, right, (((1,), (1,)), ((), ())), precision=PRECISION, preferred_element_type=jnp.float32
-    )
-
-
-def dot(left, right):
-    return lax.dot_general(
-        left, right, (((1,), (0,)), ((), ())), precision=PRECISION, preferred_element_type=jnp.float32
+        jnp.concatenate([left_high, left_high, left_low], axis=1),
+        jnp.concatenate([right_high, right_low, right_high], axis=axis),
+        (((1,), (axis,)), ((), ())),
+        preferred_element_type=jnp.float32,
     )
 
 
@@ -28,29 +31,21 @@
 
 
 def put_table(table, piece, row, chips, parity, core):
-    for value in range(2):
-        at = row + 16 * value
-        real, imag = piece[:, at : at + 8, :], piece[:, at + 8 : at + 16, :]
-        low = lax.broadcasted_iota(jnp.int32, real.shape, 1) < 4
-        real_r, imag_r = pltpu.roll(real, 4, 1), pltpu.roll(imag, 4, 1)
-        columns = (
-            jnp.where(low, real, imag_r),
-            jnp.where(low, real_r, imag),
-            jnp.where(low, -imag, real_r),
-            jnp.where(low, -imag_r, real),
-        )
-        for spot, column in enumerate(columns):
-            at = (4 * value + spot) * LANES
-            table[chips, parity, core, :, at : at + LANES] = column
-
-
-def core_and_parity():
-    place = lax.axis_index("tensor")
-    return lax.rem(place, 2), lax.rem(place // 2, 2)
+    real, imag = piece[:, row : row + 8, :], piece[:, row + 8 : row + 16, :]
+    low = lax.broadcasted_iota(jnp.int32, real.shape, 1) < 4
+    real_r, imag_r = pltpu.roll(real, 4, 1), pltpu.roll(imag, 4, 1)
+    columns = (
+        jnp.where(low, real, imag_r),
+        jnp.where(low, real_r, imag),
+        jnp.where(low, -imag, real_r),
+        jnp.where(low, -imag_r, real),
+    )
+    for spot, column in enumerate(columns):
+        table[chips, parity, core, :, spot * LANES : (spot + 1) * LANES] = column
 
 
 def flat(table):
-    return table[...].reshape(-1, table.shape[-1])
+    return jnp.concatenate([table[value].reshape(-1, table.shape[-1]) for value in range(2)], axis=1)
 
 
 def put_rows(masked, x, row, column, flag):
@@ -70,13 +65,14 @@
         copy.start()
     for copy in copies:
         copy.wait()
-    rows = block.shape[1]
-    for k, t in enumerate((0, 1, 2 + turn())):
-        out[k * rows : (k + 1) * rows, :] = block[order[t]]
+    table, value = turn()
+    for k, (t, v) in enumerate(((0, 0), (0, 1), (1, 0), (1, 1), (2 + table, value))):
+        out[16 * k : 16 * (k + 1), :] = block[order[t], v]
 
 
 def turn():
-    return lax.rem(lax.axis_index("groups"), 2)
+    quarter = lax.rem(lax.axis_index("groups"), 4)
+    return quarter // 2, lax.rem(quarter, 2)
 
 
 def core_and_parity():
@@ -113,10 +109,11 @@
     pieces, (out, mine, one, two, masked, state) = refs[:6], refs[6:]
     for piece, chips, parity, core in spots(pieces):
         for step, table in enumerate((one, two)):
-            put_table(table, piece, 32 * step, chips, parity, core)
+            for value in range(2):
+                put_table(table.at[value], piece, 32 * step + 16 * value, chips, parity, core)
         mine[chips, parity, core] = piece[:, 64:, :]
     slices = out.shape[1] // 4
-    merged = dot_t(flat(one), start[...])
+    merged = product(flat(one), start[...], 1)
     for pair in range(slices // 2):
         state[pair] = merged[:, pair * LANES : (pair + 1) * LANES]
     count = merged.shape[0] // 8
@@ -129,17 +126,20 @@
             odd = jnp.where(low, pltpu.roll(a, HALF, 1), b)
             put_rows(masked, even, count * 2 * pair, column, flags[slices + 2 * pair : slices + 2 * pair + 1, :])
             put_rows(masked, odd, count * (2 * pair + 1), column, flags[slices + 2 * pair + 1 : slices + 2 * pair + 2, :])
-    merged = dot_t(flat(two), masked[...])
+    merged = product(flat(two), masked[...], 1)
     for pair in range(slices // 2):
         x = merged[:, pair * LANES : (pair + 1) * LANES]
         out[:, 8 * pair : 8 * pair + 8, :] = x.reshape(count, 8, LANES)
 
 
-def second_kernel(flags, moved, mine, other, out, tables, masked, sums, right, last):
-    for piece, spot in ((mine, turn()), (other, 1 - turn())):
-        for k in range(4):
-            parity, core = divmod(k, 2)
-            put_table(tables.at[spot], piece.at[:, parity, core], 0, slice(0, piece.shape[0]), parity, core)
+def second_kernel(flags, moved, *refs):
+    quarters, (out, tables, masked, sums, right, last) = refs[:4], refs[4:]
+    table, value = turn()
+    for k, piece in enumerate(quarters):
+        spot = tables.at[(1 - table) if k % 2 else table, (1 - value) if k // 2 else value]
+        for parity in range(2):
+            for core in range(2):
+                put_table(spot, piece.at[:, parity, core], 0, slice(0, piece.shape[0]), parity, core)
     three, four = tables.at[0], tables.at[1]
     pairs = masked.shape[1] // LANES
     count = moved.shape[0] // (8 * pairs)
@@ -157,7 +157,7 @@
             zero = jnp.zeros_like(x)
             masked[count * j : count * (j + 1), at : at + LANES] = jnp.where(one, zero, x)
             masked[count * (8 + j) : count * (9 + j), at : at + LANES] = jnp.where(one, x, zero)
-    merged = dot(flat(three), masked[...])
+    merged = product(flat(three), masked[...], 0)
     for value in range(2):
         total = jnp.zeros((merged.shape[0], LANES), jnp.float32)
         for pair in range(pairs):
@@ -173,7 +173,7 @@
             at = (4 * value + column) * LANES
             right[0:count, at : at + LANES] = x
             right[count : 2 * count, at : at + LANES] = x
-    last[...] = dot_t(flat(four), right[...])
+    last[...] = product(flat(four), right[...], 1)
     for column in range(4):
         a = last[pl.ds(2 * column, count, stride=8), :]
         b = last[pl.ds(2 * column + 1, count, stride=8), :]
@@ -228,13 +228,13 @@
     middle = entries // contract
     halves = contract // LANES
     block = branches.transpose(0, 1, 2, 4, 3).reshape(steps, n_values, parts, width, halves, LANES)
-    block = block.transpose(0, 1, 2, 4, 3, 5).reshape(steps, n_values * parts * halves * width, LANES)
+    block = block.transpose(0, 1, 2, 4, 3, 5).reshape(steps, n_values, -1, LANES)
 
     stem = stem_field.reshape(slices, parts, middle * halves, LANES).transpose(0, 2, 1, 3).reshape(-1, LANES)
-    part_rows = block.shape[1]
+    part_rows = parts * halves * width
     picked = pl.pallas_call(
         pick_kernel,
-        out_shape=jax.ShapeDtypeStruct((3 * part_rows, LANES), jnp.float32),
+        out_shape=jax.ShapeDtypeStruct((5 * part_rows, LANES), jnp.float32),
         in_specs=[pl.BlockSpec(memory_space=pl.ANY)] * 2,
         out_specs=pl.BlockSpec(memory_space=pltpu.VMEM),
         scratch_shapes=[
@@ -247,7 +247,7 @@
 
     rows = shards * 2 * width
     deep = n_values * parts * contract
-    table = (shards // 4, 2, 2, 2 * width, deep)
+    table = (n_values, shards // 4, 2, 2, 2 * width, parts * contract)
     lanes = slices * middle
     flops = 2 * 2 * rows * deep * lanes
     pairs = slices // 2
@@ -263,14 +263,20 @@
         (jnp.float32, jnp.float32),
     )(flags, start, *pieces)
     moved = lax.all_to_all(merged, "tensor", split_axis=0, concat_axis=0, tiled=True)
-    other = lax.ppermute(mine, "groups", [(g, g ^ 1) for g in range(lax.axis_size("groups"))])
+    groups = lax.axis_size("groups")
+
+    def trade(x, bit):
+        return lax.ppermute(x, "groups", [(g, g ^ bit) for g in range(groups)])
+
+    other = trade(mine, 2)
+    quarters = (mine, other, trade(mine, 1), trade(other, 1))
     summed = local_call(
         second_kernel,
         (shards * 4, LANES),
         [(2, *table), (deep, lanes), (2, rows, LANES), (2 * middle, deep), (rows, LANES)],
-        "vvvv",
+        "v" * 6,
         flops,
-    )(flags, moved.reshape(-1, LANES), mine, other)
+    )(flags, moved.reshape(-1, LANES), *quarters)
     final = lax.all_to_all(summed.reshape(shards, 4, LANES), "tensor", split_axis=0, concat_axis=0, tiled=True)
     out = local_call(last_kernel, (middle * halves * parts, LANES), [], "v", 1000)(final.reshape(-1, LANES))
     return out.reshape(middle * halves, parts, LANES).transpose(1, 0, 2).reshape(parts, entries)

time: 199 us -> 196 us (0.985)
  waiting for transfers between devices: 63.4 us -> 60.5 us
    ppermute x1 -> x3, starting transfers between devices: 1.81 us -> 4.49 us  [trade(): return lax.ppermute(x, 'groups', [(g, g ^ bit) for g in range(groups)])]
    ppermute x1 -> x3, waiting for transfers between devices: 22 us -> 20 us  [trade(): return lax.ppermute(x, 'groups', [(g, g ^ bit) for g in range(groups)])]
  transfers between devices with their start and end apart: 7 -> 9, of which waited for: 4 -> 5; matrix products, arithmetic and copies ran while one was open for 0% -> 0% of each run, Pallas kernels for 0% -> 0%
where the time goes in v3:
time: 196 us; the launch traced here: 195 us
  blocking collectives  88.6 us (45%)
  waiting for transfers between devices  60.5 us (31%)
  starting transfers between devices  33.9 us (17%)
  Pallas kernels  12.2 us (6%)
    all_gather x1, blocking collectives, exchange(): own = lax.all_gather(block, 'tensor', axis_index_groups=rings)  51.7 us
    all_to_all x1, waiting for transfers between devices, per_device(): lax.all_to_all(merged, 'tensor', split_axis=0, concat_axis=0, tiled=True)  39.4 us
    all_to_all x1, blocking collectives, per_device(): lax.all_to_all(summed.reshape(shards, 4, LANES), 'tensor', split_axis=0,...  36.9 us
    ppermute x3, waiting for transfers between devices, trade(): return lax.ppermute(x, 'groups', [(g, g ^ bit) for g in range(groups)])  20 us
    ppermute x5, starting transfers between devices, send(): lax.ppermute(x, 'tensor', [(i, (i + 2 * chips) % shards ^ cross) for i in...  17.7 us
    all_to_all x1, starting transfers between devices, per_device(): lax.all_to_all(merged, 'tensor', split_axis=0, concat_axis=0, tiled=True)  11.7 us
    pallas_call x1, Pallas kernels, per_device(): local_call(first_kernel, [(shards, 8 * pairs, LANES), (shards // 4, 2, 2,...  4.96 us
    ppermute x3, starting transfers between devices, trade(): return lax.ppermute(x, 'groups', [(g, g ^ bit) for g in range(groups)])  4.49 us
  transfers between devices with their start and end apart: 9, of which 5 were waited for; matrix products, arithmetic and copies ran while one was open for 0% of the time, Pallas kernels for 0%

profile of v3, /device:TPU:37, one launch (start us, length us, event | category | flops | bytes accessed | tf_op | source)
XLA Modules:
  0.0 195.4 jit_solution(2780179047699498739)
XLA Ops:
  0.0 1.5 shard_map.47
  1.5 51.7 %all-gather = f32[1280,128]{1,0:T(8,128)S(1)} all-gather(f32[80,128]{1,0:T(8,128)} %shard_map.47), channel_id=2, replica_groups={{0,4,8,12,16,20,24,28,32,36,40,44,48,52,56,60},{1,5,9,13,17,21,25,29,33..., dimensions={0}, use_global_device_ids=true | all-gather | bytes 696320 | tf_op jit(solution)/shard_map/all_gather | solution.py:217
  53.2 0.0 copy-start
  53.3 1.3 collective-permute-start
  54.5 0.0 copy-start.1
  54.5 1.5 collective-permute-start.1
  56.1 9.9 %collective-permute-start.2 = (f32[16,80,128]{2,1,0:T(8,128)S(1)}, f32[16,80,128]{2,1,0:T(8,128)S(1)}, u32[]{:S(2)}, u32[]{:S(2)}) collective-permute-start(f32[16,80,128]{2,1,0:T(8,128)S(1)} %bitcast.23), channel_id=1, source_target_pairs={{0,1},{1,0},{2,3},{3,2},{4,5},{5,4},{6,7},{7,6},{8,9},{9,8},{10,11... | collective-permute-start | bytes 1966088 | tf_op jit(solution)/shard_map/ppermute | solution.py:212
  65.9 0.0 collective-permute-done.refs_1_
  66.0 5.0 %collective-permute-start.3 = (f32[8,80,128]{2,1,0:T(8,128)S(1)}, f32[8,80,128]{2,1,0:T(8,128)S(1)}, u32[]{:S(2)}, u32[]{:S(2)}) collective-permute-start(f32[8,80,128]{2,1,0:T(8,128)S(1)} %collective-permute-done.refs_1_), channel_id=1, source_target_pairs={{0,1},{1,0},{2,3},{3,2},{4,5},{5,4},{6,7},{7,6},{8,9},{9,8},{10,11... | collective-permute-start | bytes 983048 | tf_op jit(solution)/shard_map/ppermute | solution.py:212
  71.0 0.0 collective-permute-done.1.refs_2_
  71.0 0.0 collective-permute-start.4
  71.0 0.0 copy-done
  71.0 0.0 copy-done.1
  71.0 0.7 shard_map.46
  71.7 0.5 collective-permute-done.3.refs_4_
  72.2 0.5 collective-permute-done.4.refs_5_
  72.7 0.0 collective-permute-done.2.refs_3_
  72.7 5.0 %shard_map.48 = (f32[64,16,128]{2,1,0:T(8,128)}, f32[16,2,2,16,128]{4,3,2,1,0:T(8,128)S(1)}) custom-call(s32[24,128]{1,0:T(8,128)S(1)} %get-tuple-element.9.flags, f32[256,1024]{1,0:T(8,128)S(1)} %get-tuple-element.10.start, f32[16,80,128]{2,1,0:T(8,128)S(1)} %bitcast.24, f32[8,80,128]{2,1,0:T(8,128)S(1)} %collective-permute-done.refs_1_, ...), custom_call_target="tpu_custom_call" | custom-call | flops 536870912 | bytes 4194304 | tf_op jit(solution)/shard_map/pallas_call | solution.py:257
  77.7 11.7 %all-to-all-start = ((f32[64,16,128]{2,1,0:T(8,128)}), f32[64,16,128]{2,1,0:T(8,128)S(1)}, u32[]{:S(2)}, u32[]{:S(2)}) async-start(f32[64,16,128]{2,1,0:T(8,128)} %get-tuple-element.11), calls=%async_computation | async-start | bytes 1048576 | tf_op jit(solution)/shard_map/all_to_all | solution.py:265
  89.4 1.5 collective-permute-start.5
  90.9 1.5 collective-permute-start.6
  92.4 9.3 %collective-permute-done.5.refs_1_ = f32[16,2,2,16,128]{4,3,2,1,0:T(8,128)S(1)} collective-permute-done((f32[16,2,2,16,128]{4,3,2,1,0:T(8,128)S(1)}, f32[16,2,2,16,128]{4,3,2,1,0:T(8,128)S(1)}, u32[]{:S(2)}, u32[]{:S(2)}) %collective-permute-start.5) | collective-permute-done | bytes 524320 | tf_op jit(solution)/shard_map/ppermute | solution.py:269
  101.7 1.5 collective-permute-start.7
  103.2 0.0 collective-permute-done.6.refs_2_
  103.2 10.7 %collective-permute-done.7.refs_3_ = f32[16,2,2,16,128]{4,3,2,1,0:T(8,128)S(1)} collective-permute-done((f32[16,2,2,16,128]{4,3,2,1,0:T(8,128)S(1)}, f32[16,2,2,16,128]{4,3,2,1,0:T(8,128)S(1)}, u32[]{:S(2)}, u32[]{:S(2)}) %collective-permute-start.7) | collective-permute-done | bytes 524320 | tf_op jit(solution)/shard_map/ppermute | solution.py:269
  113.9 39.4 %all-to-all-done = f32[64,16,128]{2,1,0:T(8,128)S(1)} async-done(((f32[64,16,128]{2,1,0:T(8,128)}), f32[64,16,128]{2,1,0:T(8,128)S(1)}, u32[]{:S(2)}, u32[]{:S(2)}) %all-to-all-start) | async-done | bytes 524320 | tf_op jit(solution)/shard_map/all_to_all | solution.py:265
  153.4 4.3 %shard_map.49 = f32[256,128]{1,0:T(8,128)S(1)} custom-call(s32[24,128]{1,0:T(8,128)S(1)} %get-tuple-element.9.flags, f32[1024,128]{1,0:T(8,128)S(1)} %bitcast.25, f32[16,2,2,16,128]{4,3,2,1,0:T(8,128)S(1)} %get-tuple-element.12.refs_0_, f32[16,2,2,16,128]{4,3,2,1,0:T(8,128)S(1)} %collective-permute-done.5.refs_1_, ...), custom_call_target="tpu_custom_call" | custom-call | flops 536870912 | bytes 4194304 | tf_op jit(solution)/shard_map/pallas_call | solution.py:273
  157.7 36.9 %all_to_all.10 = f32[64,4,128]{2,1,0:T(4,128)S(1)} all-to-all(f32[64,4,128]{2,1,0:T(4,128)S(1)} %bitcast.28), channel_id=1, replica_groups=mesh['groups'=4,'tensor'=64] {'tensor'}, dimensions={0} | all-to-all | bytes 262144 | tf_op jit(solution)/shard_map/all_to_all | solution.py:280
  194.5 0.8 shard_map.50
  (1 shorter events, 0.0 us)
Async XLA Ops:
  53.2 17.8 %copy-start = (f32[4,2,16384]{2,1,0:T(2,128)S(1)}, f32[4,2,16384]{2,1,0:T(2,128)}, u32[]{:S(2)}) copy-start(f32[4,2,16384]{2,1,0:T(2,128)} %param.4) | copy-start | bytes 1572868
  53.3 12.7 %collective-permute-start = (f32[8,80,128]{2,1,0:T(8,128)S(1)}, f32[8,80,128]{2,1,0:T(8,128)S(1)}, u32[]{:S(2)}, u32[]{:S(2)}) collective-permute-start(f32[8,80,128]{2,1,0:T(8,128)S(1)} %bitcast.30), channel_id=1, source_target_pairs={{0,2},{1,3},{2,4},{3,5},{4,6},{5,7},{6,8},{7,9},{8,10},{9,11},{10,... | collective-permute-start | bytes 983048 | tf_op jit(solution)/shard_map/ppermute | solution.py:212
  54.5 16.5 %copy-start.1 = (s32[4,4]{1,0:T(4,128)S(1)}, s32[4,4]{1,0:T(4,128)}, u32[]{:S(2)}) copy-start(s32[4,4]{1,0:T(4,128)} %values.1) | copy-start | bytes 196
  54.5 16.5 %collective-permute-start.1 = (f32[8,80,128]{2,1,0:T(8,128)S(1)}, f32[8,80,128]{2,1,0:T(8,128)S(1)}, u32[]{:S(2)}, u32[]{:S(2)}) collective-permute-start(f32[8,80,128]{2,1,0:T(8,128)S(1)} %bitcast.29), channel_id=1, source_target_pairs={{0,62},{1,63},{2,0},{3,1},{4,2},{5,3},{6,4},{7,5},{8,6},{9,7},{10,... | collective-permute-start | bytes 983048 | tf_op jit(solution)/shard_map/ppermute | solution.py:212
  56.1 16.7 %collective-permute-start.2 = (f32[16,80,128]{2,1,0:T(8,128)S(1)}, f32[16,80,128]{2,1,0:T(8,128)S(1)}, u32[]{:S(2)}, u32[]{:S(2)}) collective-permute-start(f32[16,80,128]{2,1,0:T(8,128)S(1)} %bitcast.23), channel_id=1, source_target_pairs={{0,1},{1,0},{2,3},{3,2},{4,5},{5,4},{6,7},{7,6},{8,9},{9,8},{10,11... | collective-permute-start | bytes 1966088 | tf_op jit(solution)/shard_map/ppermute | solution.py:212
  66.0 6.3 %collective-permute-start.3 = (f32[8,80,128]{2,1,0:T(8,128)S(1)}, f32[8,80,128]{2,1,0:T(8,128)S(1)}, u32[]{:S(2)}, u32[]{:S(2)}) collective-permute-start(f32[8,80,128]{2,1,0:T(8,128)S(1)} %collective-permute-done.refs_1_), channel_id=1, source_target_pairs={{0,1},{1,0},{2,3},{3,2},{4,5},{5,4},{6,7},{7,6},{8,9},{9,8},{10,11... | collective-permute-start | bytes 983048 | tf_op jit(solution)/shard_map/ppermute | solution.py:212
  71.0 1.7 collective-permute-start.4
  77.7 75.7 %all-to-all-start = ((f32[64,16,128]{2,1,0:T(8,128)}), f32[64,16,128]{2,1,0:T(8,128)S(1)}, u32[]{:S(2)}, u32[]{:S(2)}) async-start(f32[64,16,128]{2,1,0:T(8,128)} %get-tuple-element.11), calls=%async_computation | async-start | bytes 1048576 | tf_op jit(solution)/shard_map/all_to_all | solution.py:265
  89.4 12.3 %collective-permute-start.5 = (f32[16,2,2,16,128]{4,3,2,1,0:T(8,128)S(1)}, f32[16,2,2,16,128]{4,3,2,1,0:T(8,128)S(1)}, u32[]{:S(2)}, u32[]{:S(2)}) collective-permute-start(f32[16,2,2,16,128]{4,3,2,1,0:T(8,128)S(1)} %get-tuple-element.12.refs_0_), channel_id=1, source_target_pairs={{0,128},{64,192},{128,0},{192,64},{1,129},{65,193},{129,1},{193,65... | collective-permute-start | bytes 1572872 | tf_op jit(solution)/shard_map/ppermute | solution.py:269
  90.9 12.3 %collective-permute-start.6 = (f32[16,2,2,16,128]{4,3,2,1,0:T(8,128)S(1)}, f32[16,2,2,16,128]{4,3,2,1,0:T(8,128)S(1)}, u32[]{:S(2)}, u32[]{:S(2)}) collective-permute-start(f32[16,2,2,16,128]{4,3,2,1,0:T(8,128)S(1)} %get-tuple-element.12.refs_0_), channel_id=1, source_target_pairs={{0,64},{64,0},{128,192},{192,128},{1,65},{65,1},{129,193},{193,129... | collective-permute-start | bytes 1572872 | tf_op jit(solution)/shard_map/ppermute | solution.py:269
  101.7 12.2 %collective-permute-start.7 = (f32[16,2,2,16,128]{4,3,2,1,0:T(8,128)S(1)}, f32[16,2,2,16,128]{4,3,2,1,0:T(8,128)S(1)}, u32[]{:S(2)}, u32[]{:S(2)}) collective-permute-start(f32[16,2,2,16,128]{4,3,2,1,0:T(8,128)S(1)} %collective-permute-done.5.refs_1_), channel_id=1, source_target_pairs={{0,64},{64,0},{128,192},{192,128},{1,65},{65,1},{129,193},{193,129... | collective-permute-start | bytes 1572872 | tf_op jit(solution)/shard_map/ppermute | solution.py:269
